TPU v7x, 32 devices: a whole 2x2x4 slice. The times are simulated.
32 devices in a mesh: rep: 4 (over z), inst: 8 (over y, x, core).
Axes of the slice: x: 2, y: 2, z: 4, core: 2. Of those that a mesh axis runs over, the one named last changes fastest.
Arguments:
- acts: bfloat16 [32768, 4096], P(('rep', 'inst')), may hold values from -6 to 6
- grad_keys: bfloat16 [32768, 1024], P(('rep', 'inst')), may hold values from -0.0625 to 0.0625
- grad_values: bfloat16 [32768, 1024], P(('rep', 'inst')), may hold values from -0.0625 to 0.0625
- grad_logits: bfloat16 [8, 32768], P(None, ('rep', 'inst')), may hold values from -0.0625 to 0.0625
- order: int32 [32], replicated, may hold values from 0 to 31, each once
- bucket_param: float32 [4, 2048, 1024], P(None, 'inst'), may hold values from -6 to 6
- bucket_m: float32 [4, 2048, 1024], P(None, 'inst'), may hold values from -6 to 6
- bucket_v: float32 [4, 2048, 1024], P(None, 'inst'), may hold values from 0.25 to 4
- router_param: float32 [32, 1024], P('inst'), may hold values from -6 to 6
- router_m: float32 [32, 1024], P('inst'), may hold values from -6 to 6
- router_v: float32 [32, 1024], P('inst'), may hold values from 0.25 to 4
Outputs:
- new_param: float32 [4, 2048, 1024], P(None, 'inst')
- new_moment: float32 [4, 2048, 1024], P(None, 'inst')
- new_second: float32 [4, 2048, 1024], P(None, 'inst')
- router_new_param: float32 [32, 1024], P('inst')
- router_new_moment: float32 [32, 1024], P('inst')
- router_new_second: float32 [32, 1024], P('inst')
Inputs may be any that keep to these rules, and one draw needn't show every extreme that they name: order is a permutation of the 32 row blocks; entries with k * 8 <= s < (k + 1) * 8 fill bucket k.
All inputs are finite; a program needn't handle non-finite values.
Results may differ from a plain program's by a relative error of at most 0.0003.
Values sent between devices are 32-bit elements; how exact they have to be, the bound alone decides.
A program may use at most 256 MiB of HBM per device.

v0:
```python
import jax
import jax.numpy as jnp
from jax import lax
from jax.sharding import PartitionSpec as P

BUCKETS = 4
BLOCK_ROWS = 256
beta_first = 0.9
beta_second = 0.95
step_rate = 0.05
decay_rate = 0.1
epsilon = 1e-08
correct_first = 1.0 - 0.9**10
correct_second = 1.0 - 0.95**10


def contract(left, right):
    return lax.dot_general(
        left, right, (((0,), (0,)), ((), ())), preferred_element_type=jnp.float32
    )


def adamw(grad, param, moment, second):
    moment_new = beta_first * moment + (1.0 - beta_first) * grad
    second_new = beta_second * second + (1.0 - beta_second) * grad * grad
    ratio = moment_new / correct_first / (jnp.sqrt(second_new / correct_second) + epsilon)
    param_new = param - step_rate * (ratio + decay_rate * param)
    return (param_new, moment_new, second_new)


def owner_step(term, param, moment, second):
    share = lax.psum_scatter(term, "inst", scatter_dimension=0, tiled=True)
    total = lax.psum(share, "rep")
    return adamw(total, param, moment, second)


def on_device(
    acts,
    grad_keys,
    grad_values,
    grad_logits,
    order,
    bucket_param,
    bucket_m,
    bucket_v,
    router_param,
    router_m,
    router_v,
):
    per_bucket = order.shape[0] // BUCKETS
    weight_rows = jnp.concatenate([contract(acts, grad_keys), contract(acts, grad_values)], axis=0)
    params_out = []
    moments_out = []
    seconds_out = []
    for bucket in range(BUCKETS):
        pieces = []
        for slot in range(per_bucket):
            block = order[bucket * per_bucket + slot]
            pieces.append(lax.dynamic_slice_in_dim(weight_rows, block * BLOCK_ROWS, BLOCK_ROWS, 0))
        term = jnp.concatenate(pieces, axis=0)
        fresh = owner_step(term, bucket_param[bucket], bucket_m[bucket], bucket_v[bucket])
        params_out.append(fresh[0])
        moments_out.append(fresh[1])
        seconds_out.append(fresh[2])
    router_term = jnp.dot(grad_logits, acts, preferred_element_type=jnp.float32)
    router_term = router_term.reshape(-1, router_param.shape[1])
    router_share = lax.psum_scatter(router_term, "inst", scatter_dimension=0, tiled=True)
    router_total = lax.psum(router_share, "rep")
    router_fresh = adamw(router_total, router_param, router_m, router_v)
    return (
        jnp.stack(params_out),
        jnp.stack(moments_out),
        jnp.stack(seconds_out),
        router_fresh[0],
        router_fresh[1],
        router_fresh[2],
    )


def solution(mesh):
    return jax.shard_map(
        on_device,
        mesh=mesh,
        in_specs=(
            P(("rep", "inst"), None),
            P(("rep", "inst"), None),
            P(("rep", "inst"), None),
            P(None, ("rep", "inst")),
            P(),
            P(None, "inst", None),
            P(None, "inst", None),
            P(None, "inst", None),
            P("inst", None),
            P("inst", None),
            P("inst", None),
        ),
        out_specs=(
            P(None, "inst", None),
            P(None, "inst", None),
            P(None, "inst", None),
            P("inst", None),
            P("inst", None),
            P("inst", None),
        ),
        check_vma=False,
    )
```

profile of v0, /device:TPU:0, one launch (start us, length us, event | category | flops | bytes accessed | tf_op | source)
XLA Modules:
  0.0 603.0 jit_solution(1667637888820862590)
XLA Ops:
  7.2 1.8 fusion.91
  14.1 2.1 fusion.90
  18.2 14.8 %fusion.92 = f32[4096,1024]{1,0:T(8,128)} fusion(bf16[1024,4096]{1,0:T(8,128)(2,1)} %param.11, bf16[1024,1024]{1,0:T(8,128)(2,1)S(1)} %copy-done), kind=kOutput, calls=%fused_computation.178 | convolution fusion | flops 8589934592 | bytes 27262976 | tf_op jit(solution)/shard_map/dot_general | solution.py:18
  33.0 11.5 %fusion.93 = f32[4096,1024]{1,0:T(8,128)} fusion(bf16[1024,4096]{1,0:T(8,128)(2,1)S(1)} %copy-done.4, bf16[1024,1024]{1,0:T(8,128)(2,1)S(1)} %copy-done.16), kind=kOutput, calls=%fused_computation.179 | convolution fusion | flops 8589934592 | bytes 27262976 | tf_op jit(solution)/shard_map/dot_general | solution.py:18
  44.6 1.6 fusion.3
  46.2 4.4 copy-done.2
  50.6 4.8 copy-done.3
  57.1 4.1 fusion.17
  61.3 3.3 copy-done.6
  70.6 2.7 fusion.21
  73.4 3.4 fusion.23
  78.0 1.9 slice-done.13
  80.0 2.1 slice-done.2
  82.0 1.8 slice-done.3
  91.6 2.4 fusion.33
  98.5 2.8 fusion.39
  101.3 3.6 fusion.41
  105.0 1.5 slice-done.17
  115.5 2.1 fusion.49
  120.8 2.7 fusion.57
  123.6 3.8 fusion.59
  138.1 4.6 fusion.94
  143.6 70.3 %reduce-scatter.7.cloned.1.call-done = f32[256,1024]{1,0:T(8,128)} async-done(((f32[2048,1024]{1,0:T(8,128)}), f32[256,1024]{1,0:T(8,128)}) %reduce-scatter.7.cloned.1.call-update) | async-done | bytes 1048592 | tf_op jit(solution)/shard_map/reduce_scatter | solution.py:32
  213.9 75.0 %reduce-scatter.9.cloned.1.call-done = f32[256,1024]{1,0:T(8,128)} async-done(((f32[2048,1024]{1,0:T(8,128)}), f32[256,1024]{1,0:T(8,128)}) %reduce-scatter.9.cloned.1.call-update) | async-done | bytes 1048592 | tf_op jit(solution)/shard_map/reduce_scatter | solution.py:32
  288.9 74.8 %reduce-scatter.11.cloned.1.call-done = f32[256,1024]{1,0:T(8,128)} async-done(((f32[2048,1024]{1,0:T(8,128)}), f32[256,1024]{1,0:T(8,128)}) %reduce-scatter.11.cloned.1.call-update) | async-done | bytes 1048592 | tf_op jit(solution)/shard_map/reduce_scatter | solution.py:32
  365.0 55.6 %all-reduce.5.cloned.1.call-done = f32[32,1024]{1,0:T(8,128)} async-done(((f32[32,1024]{1,0:T(8,128)}), f32[32,1024]{1,0:T(8,128)}) %all-reduce.5.cloned.1.call-update) | async-done | bytes 131088
  421.4 19.5 %psum.39 = f32[4,1024]{1,0:T(4,128)S(1)} all-reduce(f32[4,1024]{1,0:T(4,128)S(1)} %constant_dynamic-slice_fusion), channel_id=1, replica_groups=mesh['rep'=4,'inst'=8] {'rep'}, use_global_device_ids=true, to_apply=%region_9.0 | all-reduce | flops 4096 | bytes 32768 | tf_op jit(solution)/shard_map/psum | solution.py:68
  441.6 136.1 %all-reduce.7.cloned.1.call-done = (f32[256,1024]{1,0:T(8,128)}, f32[256,1024]{1,0:T(8,128)}, f32[256,1024]{1,0:T(8,128)}, f32[256,1024]{1,0:T(8,128)}) async-done(((f32[256,1024]{1,0:T(8,128)}, f32[256,1024]{1,0:T(8,128)}, f32[256,1024]{1,0:T(8,128)}, f32[256,1024]{1,0:T(8,128)}), (f32[256,1024]{1,0:T(8,128)}, f32[256,1024]{1,0:T(8,128)}, f32[256,1024]{1,0:T(8,128)}, ...) | async-done | bytes 4194320 | tf_op jit(solution)/shard_map/psum | solution.py:33
  577.7 5.6 fusion.80
  585.0 4.7 fusion.79
  589.7 2.6 pad_maximum_fusion.1
  592.3 3.8 pad_maximum_fusion
  (116 shorter events, 35.4 us)
Async XLA Ops:
  7.2 11.0 %copy-start = (bf16[1024,1024]{1,0:T(8,128)(2,1)S(1)}, bf16[1024,1024]{1,0:T(8,128)(2,1)}, u32[]{:S(2)}) copy-start(bf16[1024,1024]{1,0:T(8,128)(2,1)} %param.12) | copy-start | bytes 6291460
  7.2 136.4 %reduce-scatter.5.cloned.1.call-start = ((), (), s32[]{:S(2)}) async-start(), calls=%async_computation.4 | async-start | bytes 9437184 | tf_op jit(solution)/shard_map/reduce_scatter | solution.py:32
  18.2 14.8 %copy-start.4 = (bf16[1024,4096]{1,0:T(8,128)(2,1)S(1)}, bf16[1024,4096]{1,0:T(8,128)(2,1)}, u32[]{:S(2)}) copy-start(bf16[1024,4096]{1,0:T(8,128)(2,1)} %param.11) | copy-start | bytes 25165828
  18.2 14.8 %copy-start.16 = (bf16[1024,1024]{1,0:T(8,128)(2,1)S(1)}, bf16[1024,1024]{1,0:T(8,128)(2,1)}, u32[]{:S(2)}) copy-start(bf16[1024,1024]{1,0:T(8,128)(2,1)} %param.13) | copy-start | bytes 6291460
  44.6 10.9 %copy-start.3 = (f32[4096,1024]{1,0:T(8,128)S(1)}, f32[4096,1024]{1,0:T(8,128)}, u32[]{:S(2)}) copy-start(f32[4096,1024]{1,0:T(8,128)} %fusion.93) | copy-start | bytes 50331652
  64.6 149.4 %reduce-scatter.7.cloned.1.call-start = ((), (), s32[]{:S(2)}) async-start(), calls=%async_computation.5 | async-start | bytes 9437184 | tf_op jit(solution)/shard_map/reduce_scatter | solution.py:32
  70.6 7.4 %slice-start.12 = ((s8[16777216]{0:T(1024)(128)(4,1)}), s8[4194304]{0:T(1024)(128)(4,1)S(1)}, s32[]{:S(2)}) async-start(s8[16777216]{0:T(1024)(128)(4,1)} %bitcast.161), calls=%async_computation.22 | async-start | bytes 8388608
  70.6 9.3 %slice-start.13 = ((s8[16777216]{0:T(1024)(128)(4,1)}), s8[4194304]{0:T(1024)(128)(4,1)S(1)}, s32[]{:S(2)}) async-start(s8[16777216]{0:T(1024)(128)(4,1)} %bitcast.161), calls=%async_computation.23 | async-start | bytes 8388608
  73.4 8.6 %slice-start.2 = ((s8[16777216]{0:T(1024)(128)(4,1)}), s8[4194304]{0:T(1024)(128)(4,1)S(1)}, s32[]{:S(2)}) async-start(s8[16777216]{0:T(1024)(128)(4,1)} %bitcast.155), calls=%async_computation.12 | async-start | bytes 8388608
  73.4 10.5 %slice-start.3 = ((s8[16777216]{0:T(1024)(128)(4,1)}), s8[4194304]{0:T(1024)(128)(4,1)S(1)}, s32[]{:S(2)}) async-start(s8[16777216]{0:T(1024)(128)(4,1)} %bitcast.155), calls=%async_computation.13 | async-start | bytes 8388608
  73.4 11.8 %slice-start.14 = ((s8[16777216]{0:T(1024)(128)(4,1)}), s8[4194304]{0:T(1024)(128)(4,1)S(1)}, s32[]{:S(2)}) async-start(s8[16777216]{0:T(1024)(128)(4,1)} %bitcast.161), calls=%async_computation.24 | async-start | bytes 8388608
  73.4 13.2 %slice-start.15 = ((s8[16777216]{0:T(1024)(128)(4,1)}), s8[4194304]{0:T(1024)(128)(4,1)S(1)}, s32[]{:S(2)}) async-start(s8[16777216]{0:T(1024)(128)(4,1)} %bitcast.161), calls=%async_computation.25 | async-start | bytes 8388608
  94.0 194.9 %reduce-scatter.9.cloned.1.call-start = ((), (), s32[]{:S(2)}) async-start(), calls=%async_computation.6 | async-start | bytes 9437184 | tf_op jit(solution)/shard_map/reduce_scatter | solution.py:32
  98.5 8.0 %slice-start.17 = ((s8[16777216]{0:T(1024)(128)(4,1)}), s8[4194304]{0:T(1024)(128)(4,1)S(1)}, s32[]{:S(2)}) async-start(s8[16777216]{0:T(1024)(128)(4,1)} %bitcast.163), calls=%async_computation.27 | async-start | bytes 8388608
  101.3 7.9 %slice-start.7 = ((s8[16777216]{0:T(1024)(128)(4,1)}), s8[4194304]{0:T(1024)(128)(4,1)S(1)}, s32[]{:S(2)}) async-start(s8[16777216]{0:T(1024)(128)(4,1)} %bitcast.157), calls=%async_computation.17 | async-start | bytes 8388608
  101.3 9.1 %slice-start.18 = ((s8[16777216]{0:T(1024)(128)(4,1)}), s8[4194304]{0:T(1024)(128)(4,1)S(1)}, s32[]{:S(2)}) async-start(s8[16777216]{0:T(1024)(128)(4,1)} %bitcast.163), calls=%async_computation.28 | async-start | bytes 8388608
  101.3 10.4 %slice-start.19 = ((s8[16777216]{0:T(1024)(128)(4,1)}), s8[4194304]{0:T(1024)(128)(4,1)S(1)}, s32[]{:S(2)}) async-start(s8[16777216]{0:T(1024)(128)(4,1)} %bitcast.163), calls=%async_computation.29 | async-start | bytes 8388608
  117.7 246.1 %reduce-scatter.11.cloned.1.call-start = ((), (), s32[]{:S(2)}) async-start(), calls=%async_computation.7 | async-start | bytes 9437184 | tf_op jit(solution)/shard_map/reduce_scatter | solution.py:32
  120.8 6.6 %slice-start.8 = ((s8[16777216]{0:T(1024)(128)(4,1)}), s8[4194304]{0:T(1024)(128)(4,1)S(1)}, s32[]{:S(2)}) async-start(s8[16777216]{0:T(1024)(128)(4,1)} %bitcast.159), calls=%async_computation.18 | async-start | bytes 8388608
  120.8 7.9 %slice-start.21 = ((s8[16777216]{0:T(1024)(128)(4,1)}), s8[4194304]{0:T(1024)(128)(4,1)S(1)}, s32[]{:S(2)}) async-start(s8[16777216]{0:T(1024)(128)(4,1)} %bitcast.165), calls=%async_computation.31 | async-start | bytes 8388608
  123.6 7.6 %slice-start.11 = ((s8[16777216]{0:T(1024)(128)(4,1)}), s8[4194304]{0:T(1024)(128)(4,1)S(1)}, s32[]{:S(2)}) async-start(s8[16777216]{0:T(1024)(128)(4,1)} %bitcast.159), calls=%async_computation.21 | async-start | bytes 8388608
  123.6 8.8 %slice-start.22 = ((s8[16777216]{0:T(1024)(128)(4,1)}), s8[4194304]{0:T(1024)(128)(4,1)S(1)}, s32[]{:S(2)}) async-start(s8[16777216]{0:T(1024)(128)(4,1)} %bitcast.165), calls=%async_computation.32 | async-start | bytes 8388608
  123.6 10.0 %slice-start.23 = ((s8[16777216]{0:T(1024)(128)(4,1)}), s8[4194304]{0:T(1024)(128)(4,1)S(1)}, s32[]{:S(2)}) async-start(s8[16777216]{0:T(1024)(128)(4,1)} %bitcast.165), calls=%async_computation.33 | async-start | bytes 8388608
  137.4 226.3 %copy-start.17 = (u32[32]{0:T(128)S(1)}, u32[32]{0:T(128)}, u32[]{:S(2)}) copy-start(u32[32]{0:T(128)} %constant.74) | copy-start | bytes 388
  137.5 303.5 %copy-start.13 = (f32[4,1024]{1,0:T(4,128)S(1)}, f32[4,1024]{1,0:T(4,128)}, u32[]{:S(2)}) copy-start(f32[4,1024]{1,0:T(4,128)} %param.19) | copy-start | bytes 49156
  137.5 303.5 %copy-start.14 = (f32[4,1024]{1,0:T(4,128)S(1)}, f32[4,1024]{1,0:T(4,128)}, u32[]{:S(2)}) copy-start(f32[4,1024]{1,0:T(4,128)} %param.20) | copy-start | bytes 49156
  137.5 303.5 %copy-start.15 = (f32[4,1024]{1,0:T(4,128)S(1)}, f32[4,1024]{1,0:T(4,128)}, u32[]{:S(2)}) copy-start(f32[4,1024]{1,0:T(4,128)} %param.21) | copy-start | bytes 49156
  137.5 283.2 %all-reduce.5.cloned.1.call-start = ((), (), s32[]{:S(2)}) async-start(), calls=%async_computation.8 | async-start | bytes 262144
  143.5 434.2 %all-reduce.7.cloned.1.call-start = ((), (), s32[]{:S(2)}) async-start(), calls=%async_computation.9 | async-start | bytes 8388608 | tf_op jit(solution)/shard_map/psum | solution.py:33
  577.7 6.7 %copy-start.9 = (f32[256,1024]{1,0:T(8,128)S(1)}, f32[256,1024]{1,0:T(8,128)}, u32[]{:S(2)}) copy-start(f32[256,1024]{1,0:T(8,128)} %get-tuple-element.7) | copy-start | bytes 3145732
  577.7 7.0 %copy-start.10 = (f32[256,1024]{1,0:T(8,128)S(1)}, f32[256,1024]{1,0:T(8,128)}, u32[]{:S(2)}) copy-start(f32[256,1024]{1,0:T(8,128)} %get-tuple-element.8) | copy-start | bytes 3145732
  577.7 7.3 %copy-start.11 = (f32[256,1024]{1,0:T(8,128)S(1)}, f32[256,1024]{1,0:T(8,128)}, u32[]{:S(2)}) copy-start(f32[256,1024]{1,0:T(8,128)} %get-tuple-element.9) | copy-start | bytes 3145732
  (16 other events, 90.2 us)
Sparse Core Ops, SparseCore 0:
  64.7 74.2 reduce-scatter.4
  142.4 71.4 reduce-scatter.6
  217.4 71.4 reduce-scatter.8
  292.2 71.4 reduce-scatter.10
  367.2 53.3 all-reduce.4
  423.1 154.5 all-reduce.6
where the time goes:
time: 604 us; the launch traced here: 603 us
  waiting for transfers between devices  412 us (68%)
  other arithmetic  61.2 us (10%)
  local copies, waits for them, and re-layouts  43.5 us (7%)
  between operations  35.4 us (6%)
  matrix products  31 us (5%)
  blocking collectives  19.5 us (3%)
    reduce_scatter x4, waiting for transfers between devices, owner_step(): share = lax.psum_scatter(term, 'inst', scatter_dimension=0, tiled=True)  220 us
    psum x1, waiting for transfers between devices, owner_step(): total = lax.psum(share, 'rep')  136 us
    unnamed x7, waiting for transfers between devices  55.7 us
    unnamed x86, local copies, waits for them, and re-layouts  38.9 us
    unnamed x28, other arithmetic  33.9 us
    dot_general x2, matrix products, contract(): lax.dot_general(left, right, (((0,), (0,)), ((), ())), preferred_element_...  26.3 us
    psum x1, blocking collectives, on_device(): router_total = lax.psum(router_share, 'rep')  19.5 us
  transfers between devices with their start and end apart: 6, of which 5 were waited for; matrix products, arithmetic and copies ran while one was open for 7% of the time, Pallas kernels for 0%

commit v1 on v0

--- a/solution.py
+++ b/solution.py
@@ -30,7 +30,7 @@
 
 def owner_step(term, param, moment, second):
     share = lax.psum_scatter(term, "inst", scatter_dimension=0, tiled=True)
-    total = lax.psum(share, "rep")
+    total = jnp.sum(lax.all_gather(share, "rep"), axis=0)
     return adamw(total, param, moment, second)
 
 

time: 604 us -> 780 us (1.29)
  waiting for transfers between devices: 412 us -> 582 us
  other arithmetic: 61.2 us -> 80.3 us
  local copies, waits for them, and re-layouts: 43.5 us -> 30.7 us
    all_gather x0 -> x4, waiting for transfers between devices: none -> 295 us  [owner_step(): total = jnp.sum(lax.all_gather(share, 'rep'), axis=0)]
    psum x1 -> x0, waiting for transfers between devices: 136 us -> none  [owner_step(): total = lax.psum(share, 'rep')]
    unnamed x86 -> x56, local copies, waits for them, and re-layouts: 38.9 us -> 26.1 us
    reduce_sum x0 -> x4, other arithmetic: none -> 11.8 us  [owner_step(): total = jnp.sum(lax.all_gather(share, 'rep'), axis=0)]
    reduce_scatter x4, waiting for transfers between devices: 220 us -> 231 us  [owner_step(): share = lax.psum_scatter(term, 'inst', scatter_dimension=0, tiled=True)]
    unnamed x28 -> x26, other arithmetic: 33.9 us -> 43.4 us
    unnamed x7 -> x10, waiting for transfers between devices: 55.7 us -> 56.3 us
  transfers between devices with their start and end apart: 6 -> 9, of which waited for: 5 -> 9; matrix products, arithmetic and copies ran while one was open for 7% -> 6% of each run, Pallas kernels for 0% -> 0%
where the time goes in v1:
time: 780 us; the launch traced here: 779 us
  waiting for transfers between devices  582 us (75%)
  other arithmetic  80.3 us (10%)
  between operations  34.9 us (4%)
  matrix products  30.9 us (4%)
  local copies, waits for them, and re-layouts  30.7 us (4%)
  blocking collectives  19.5 us (2%)
    all_gather x4, waiting for transfers between devices, owner_step(): total = jnp.sum(lax.all_gather(share, 'rep'), axis=0)  295 us
    reduce_scatter x4, waiting for transfers between devices, owner_step(): share = lax.psum_scatter(term, 'inst', scatter_dimension=0, tiled=True)  231 us
    unnamed x10, waiting for transfers between devices  56.3 us
    unnamed x26, other arithmetic  43.4 us
    dot_general x2, matrix products, contract(): lax.dot_general(left, right, (((0,), (0,)), ((), ())), preferred_element_...  26.3 us
    unnamed x56, local copies, waits for them, and re-layouts  26.1 us
    psum x1, blocking collectives, on_device(): router_total = lax.psum(router_share, 'rep')  19.5 us
  transfers between devices with their start and end apart: 9, of which 9 were waited for; matrix products, arithmetic and copies ran while one was open for 6% of the time, Pallas kernels for 0%

profile of v1, /device:TPU:0, one launch (start us, length us, event | category | flops | bytes accessed | tf_op | source)
XLA Modules:
  0.0 778.9 jit_solution(2265423443850858630)
XLA Ops:
  18.2 14.8 %fusion.84 = f32[4096,1024]{1,0:T(8,128)} fusion(bf16[1024,4096]{1,0:T(8,128)(2,1)} %param.11, bf16[1024,1024]{1,0:T(8,128)(2,1)S(1)} %copy-done), kind=kOutput, calls=%fused_computation.158 | convolution fusion | flops 8589934592 | bytes 27262976 | tf_op jit(solution)/shard_map/dot_general | solution.py:18
  32.9 11.6 %fusion.85 = f32[4096,1024]{1,0:T(8,128)} fusion(bf16[1024,4096]{1,0:T(8,128)(2,1)S(1)} %copy-done.4, bf16[1024,1024]{1,0:T(8,128)(2,1)S(1)} %copy-done.9), kind=kOutput, calls=%fused_computation.159 | convolution fusion | flops 8589934592 | bytes 27262976 | tf_op jit(solution)/shard_map/dot_general | solution.py:18
  44.5 2.7 fusion.3
  47.2 3.7 copy-done.2
  51.0 4.8 copy-done.3
  57.0 2.6 fusion.7
  59.5 2.6 fusion.9
  62.1 2.6 fusion.11
  67.3 2.6 fusion.15
  69.9 5.4 fusion.17
  81.3 2.7 fusion.21
  84.1 3.4 fusion.23
  112.2 2.9 fusion.39
  115.1 3.6 fusion.41
  138.2 4.6 fusion.86
  143.5 6.2 reduce-scatter.5.cloned.1.call-done
  149.8 74.9 %reduce-scatter.7.cloned.1.call-done = f32[256,1024]{1,0:T(8,128)} async-done(((f32[2048,1024]{1,0:T(8,128)}), f32[256,1024]{1,0:T(8,128)}) %reduce-scatter.7.cloned.1.call-update) | async-done | bytes 1048592 | tf_op jit(solution)/shard_map/reduce_scatter | solution.py:32
  224.8 74.9 %reduce-scatter.11.cloned.1.call-done = f32[256,1024]{1,0:T(8,128)} async-done(((f32[2048,1024]{1,0:T(8,128)}), f32[256,1024]{1,0:T(8,128)}) %reduce-scatter.11.cloned.1.call-update) | async-done | bytes 1048592 | tf_op jit(solution)/shard_map/reduce_scatter | solution.py:32
  299.7 74.8 %reduce-scatter.9.cloned.1.call-done = f32[256,1024]{1,0:T(8,128)} async-done(((f32[2048,1024]{1,0:T(8,128)}), f32[256,1024]{1,0:T(8,128)}) %reduce-scatter.9.cloned.1.call-update) | async-done | bytes 1048592 | tf_op jit(solution)/shard_map/reduce_scatter | solution.py:32
  375.8 55.6 %all-reduce.3.cloned.1.call-done = f32[32,1024]{1,0:T(8,128)} async-done(((f32[32,1024]{1,0:T(8,128)}), f32[32,1024]{1,0:T(8,128)}) %all-reduce.3.cloned.1.call-update) | async-done | bytes 131088
  432.2 19.5 %psum.7 = f32[4,1024]{1,0:T(4,128)S(1)} all-reduce(f32[4,1024]{1,0:T(4,128)S(1)} %constant_dynamic-slice_fusion), channel_id=1, replica_groups=mesh['rep'=4,'inst'=8] {'rep'}, use_global_device_ids=true, to_apply=%region_9.0 | all-reduce | flops 4096 | bytes 32768 | tf_op jit(solution)/shard_map/psum | solution.py:68
  452.3 60.8 %all-gather.9.cloned.1.call-done = f32[1024,1024]{1,0:T(8,128)} async-done(((f32[256,1024]{1,0:T(8,128)}), f32[1024,1024]{1,0:T(8,128)}) %all-gather.9.cloned.1.call-update) | async-done | bytes 4194320 | tf_op jit(solution)/shard_map/all_gather | solution.py:33
  513.2 2.7 reduce_sum.44
  515.9 77.9 %all-gather.11.cloned.1.call-done = f32[1024,1024]{1,0:T(8,128)} async-done(((f32[256,1024]{1,0:T(8,128)}), f32[1024,1024]{1,0:T(8,128)}) %all-gather.11.cloned.1.call-update) | async-done | bytes 4194320 | tf_op jit(solution)/shard_map/all_gather | solution.py:33
  593.8 2.7 reduce_sum.46
  596.5 78.1 %all-gather.15.cloned.1.call-done = f32[1024,1024]{1,0:T(8,128)} async-done(((f32[256,1024]{1,0:T(8,128)}), f32[1024,1024]{1,0:T(8,128)}) %all-gather.15.cloned.1.call-update) | async-done | bytes 4194320 | tf_op jit(solution)/shard_map/all_gather | solution.py:33
  674.6 2.7 reduce_sum.50
  677.4 78.1 %all-gather.13.cloned.1.call-done = f32[1024,1024]{1,0:T(8,128)} async-done(((f32[256,1024]{1,0:T(8,128)}), f32[1024,1024]{1,0:T(8,128)}) %all-gather.13.cloned.1.call-update) | async-done | bytes 4194320 | tf_op jit(solution)/shard_map/all_gather | solution.py:33
  755.5 3.7 reduce_sum.48
  759.2 6.7 multiply_subtract_fusion.3
  765.9 2.6 pad_maximum_fusion.2
  768.5 3.9 pad_maximum_fusion
  (96 shorter events, 47.6 us)
Async XLA Ops:
  7.2 11.0 %copy-start = (bf16[1024,1024]{1,0:T(8,128)(2,1)S(1)}, bf16[1024,1024]{1,0:T(8,128)(2,1)}, u32[]{:S(2)}) copy-start(bf16[1024,1024]{1,0:T(8,128)(2,1)} %param.12) | copy-start | bytes 6291460
  7.2 142.5 %reduce-scatter.5.cloned.1.call-start = ((), (), s32[]{:S(2)}) async-start(), calls=%async_computation.4 | async-start | bytes 9437184 | tf_op jit(solution)/shard_map/reduce_scatter | solution.py:32
  18.1 14.8 %copy-start.4 = (bf16[1024,4096]{1,0:T(8,128)(2,1)S(1)}, bf16[1024,4096]{1,0:T(8,128)(2,1)}, u32[]{:S(2)}) copy-start(bf16[1024,4096]{1,0:T(8,128)(2,1)} %param.11) | copy-start | bytes 25165828
  18.2 14.8 %copy-start.9 = (bf16[1024,1024]{1,0:T(8,128)(2,1)S(1)}, bf16[1024,1024]{1,0:T(8,128)(2,1)}, u32[]{:S(2)}) copy-start(bf16[1024,1024]{1,0:T(8,128)(2,1)} %param.13) | copy-start | bytes 6291460
  44.5 6.5 copy-start.2
  44.5 11.2 %copy-start.3 = (f32[4096,1024]{1,0:T(8,128)S(1)}, f32[4096,1024]{1,0:T(8,128)}, u32[]{:S(2)}) copy-start(f32[4096,1024]{1,0:T(8,128)} %fusion.85) | copy-start | bytes 50331652
  75.3 149.4 %reduce-scatter.7.cloned.1.call-start = ((), (), s32[]{:S(2)}) async-start(), calls=%async_computation.5 | async-start | bytes 9437184 | tf_op jit(solution)/shard_map/reduce_scatter | solution.py:32
  81.3 7.4 slice-start.8
  81.3 9.3 %slice-start.9 = ((s8[16777216]{0:T(1024)(128)(4,1)}), s8[4194304]{0:T(1024)(128)(4,1)S(1)}, s32[]{:S(2)}) async-start(s8[16777216]{0:T(1024)(128)(4,1)} %bitcast.75), calls=%async_computation.22 | async-start | bytes 8388608
  84.1 8.6 %slice-start.2 = ((s8[16777216]{0:T(1024)(128)(4,1)}), s8[4194304]{0:T(1024)(128)(4,1)S(1)}, s32[]{:S(2)}) async-start(s8[16777216]{0:T(1024)(128)(4,1)} %bitcast.71), calls=%async_computation.15 | async-start | bytes 8388608
  84.1 10.4 %slice-start.3 = ((s8[16777216]{0:T(1024)(128)(4,1)}), s8[4194304]{0:T(1024)(128)(4,1)S(1)}, s32[]{:S(2)}) async-start(s8[16777216]{0:T(1024)(128)(4,1)} %bitcast.71), calls=%async_computation.16 | async-start | bytes 8388608
  84.1 11.8 %slice-start.10 = ((s8[16777216]{0:T(1024)(128)(4,1)}), s8[4194304]{0:T(1024)(128)(4,1)S(1)}, s32[]{:S(2)}) async-start(s8[16777216]{0:T(1024)(128)(4,1)} %bitcast.75), calls=%async_computation.23 | async-start | bytes 8388608
  84.1 13.1 %slice-start.11 = ((s8[16777216]{0:T(1024)(128)(4,1)}), s8[4194304]{0:T(1024)(128)(4,1)S(1)}, s32[]{:S(2)}) async-start(s8[16777216]{0:T(1024)(128)(4,1)} %bitcast.75), calls=%async_computation.24 | async-start | bytes 8388608
  104.7 195.0 %reduce-scatter.11.cloned.1.call-start = ((), (), s32[]{:S(2)}) async-start(), calls=%async_computation.7 | async-start | bytes 9437184 | tf_op jit(solution)/shard_map/reduce_scatter | solution.py:32
  112.2 6.5 slice-start.4
  112.2 6.5 slice-start.5
  112.2 6.5 slice-start.12
  112.2 7.9 %slice-start.13 = ((s8[16777216]{0:T(1024)(128)(4,1)}), s8[4194304]{0:T(1024)(128)(4,1)S(1)}, s32[]{:S(2)}) async-start(s8[16777216]{0:T(1024)(128)(4,1)} %bitcast.77), calls=%async_computation.26 | async-start | bytes 8388608
  115.1 6.3 slice-start.6
  115.1 7.6 slice-start.7
  115.1 8.8 %slice-start.14 = ((s8[16777216]{0:T(1024)(128)(4,1)}), s8[4194304]{0:T(1024)(128)(4,1)S(1)}, s32[]{:S(2)}) async-start(s8[16777216]{0:T(1024)(128)(4,1)} %bitcast.77), calls=%async_computation.27 | async-start | bytes 8388608
  115.1 10.1 %slice-start.15 = ((s8[16777216]{0:T(1024)(128)(4,1)}), s8[4194304]{0:T(1024)(128)(4,1)S(1)}, s32[]{:S(2)}) async-start(s8[16777216]{0:T(1024)(128)(4,1)} %bitcast.77), calls=%async_computation.28 | async-start | bytes 8388608
  137.5 237.0 %reduce-scatter.9.cloned.1.call-start = ((), (), s32[]{:S(2)}) async-start(), calls=%async_computation.6 | async-start | bytes 9437184 | tf_op jit(solution)/shard_map/reduce_scatter | solution.py:32
  138.1 236.5 %copy-start.10 = (u32[32]{0:T(128)S(1)}, u32[32]{0:T(128)}, u32[]{:S(2)}) copy-start(u32[32]{0:T(128)} %constant.76) | copy-start | bytes 388
  138.1 313.6 %copy-start.6 = (f32[4,1024]{1,0:T(4,128)S(1)}, f32[4,1024]{1,0:T(4,128)}, u32[]{:S(2)}) copy-start(f32[4,1024]{1,0:T(4,128)} %param.19) | copy-start | bytes 49156
  138.1 313.6 %copy-start.7 = (f32[4,1024]{1,0:T(4,128)S(1)}, f32[4,1024]{1,0:T(4,128)}, u32[]{:S(2)}) copy-start(f32[4,1024]{1,0:T(4,128)} %param.20) | copy-start | bytes 49156
  138.1 313.6 %copy-start.8 = (f32[4,1024]{1,0:T(4,128)S(1)}, f32[4,1024]{1,0:T(4,128)}, u32[]{:S(2)}) copy-start(f32[4,1024]{1,0:T(4,128)} %param.21) | copy-start | bytes 49156
  138.1 293.3 %all-reduce.3.cloned.1.call-start = ((), (), s32[]{:S(2)}) async-start(), calls=%async_computation.12 | async-start | bytes 262144
  143.5 369.7 %all-gather.9.cloned.1.call-start = ((), (), s32[]{:S(2)}) async-start(), calls=%async_computation.8 | async-start | bytes 5242880 | tf_op jit(solution)/shard_map/all_gather | solution.py:33
  149.7 444.1 %all-gather.11.cloned.1.call-start = ((), (), s32[]{:S(2)}) async-start(), calls=%async_computation.9 | async-start | bytes 5242880 | tf_op jit(solution)/shard_map/all_gather | solution.py:33
  224.7 449.9 %all-gather.15.cloned.1.call-start = ((), (), s32[]{:S(2)}) async-start(), calls=%async_computation.11 | async-start | bytes 5242880 | tf_op jit(solution)/shard_map/all_gather | solution.py:33
  299.7 455.8 %all-gather.13.cloned.1.call-start = ((), (), s32[]{:S(2)}) async-start(), calls=%async_computation.10 | async-start | bytes 5242880 | tf_op jit(solution)/shard_map/all_gather | solution.py:33
  (4 other events, 17.0 us)
Sparse Core Ops, SparseCore 0:
  75.4 74.2 reduce-scatter.4
  153.2 71.4 reduce-scatter.6
  228.1 71.4 reduce-scatter.10
  303.0 71.4 reduce-scatter.8
  378.0 53.3 all-reduce.2
  432.8 80.2 all-gather.8
  514.7 79.0 all-gather.10
  595.4 79.2 all-gather.14
  676.2 79.2 all-gather.12
